TPU v7x, 32 devices: a whole 2x2x4 slice. The times are simulated.
32 devices in a mesh: fsdp: 4 (over z), tp: 4 (over y, x), job: 2 (over core).
Axes of the slice: x: 2, y: 2, z: 4, core: 2. Of those that a mesh axis runs over, the one named last changes fastest.
Arguments:
- slopes_in: float32 [128, 128, 1024], P('job', 'fsdp', 'tp'), parts along dimension 0, may hold values from -6 to 6
- moments_in: float32 [128, 128, 1024], P('job', 'fsdp', 'tp'), parts along dimension 0, may hold values from -6 to 6
- weights_in: float32 [128, 128, 1024], P('job', 'fsdp', 'tp'), parts along dimension 0, may hold values from -0.1875 to 0.1875
Outputs:
- new_weights: float32 [128, 128, 1024], P('job', 'fsdp', 'tp'), parts along dimension 0
- new_momentum: float32 [128, 128, 1024], P('job', 'fsdp', 'tp'), parts along dimension 0
There are 2 independent parts, one for each index of `job`. A program takes and returns all parts, laid end to end along the dimension named above; each array names one. Nothing has to cross between parts.
All inputs are finite; a program needn't handle non-finite values.
Results may differ from a plain program's by a relative error of at most 0.00019.
Values sent between devices are 32-bit elements; how exact they have to be, the bound alone decides.
A program may use at most 128 MiB of HBM per device.

v0:
```python
import jax
import jax.numpy as jnp
from jax import lax
from jax.sharding import PartitionSpec as P

ITERS = 5


hold_rate = 0.9
learn_rate = 0.8


def body(slopes_in, moments_in, weights_in):
    new_momentum = hold_rate * moments_in + slopes_in
    moved = lax.all_to_all(new_momentum, "fsdp", split_axis=0, concat_axis=1, tiled=True)
    whole = lax.all_to_all(moved, "tp", split_axis=0, concat_axis=2, tiled=True)
    iterate = whole * lax.rsqrt(jnp.sum(whole * whole, axis=(1, 2), keepdims=True) + 1e-06)
    for step in range(ITERS):
        gram = jnp.einsum("mik,mjk->mij", iterate, iterate, precision=lax.Precision.HIGHEST)
        mixed = -4.775 * gram + 2.0315 * jnp.einsum(
            "mij,mjk->mik", gram, gram, precision=lax.Precision.HIGHEST
        )
        iterate = 3.4445 * iterate + jnp.einsum(
            "mij,mjk->mik", mixed, iterate, precision=lax.Precision.HIGHEST
        )
    iterate = lax.all_to_all(iterate, "tp", split_axis=2, concat_axis=0, tiled=True)
    back = lax.all_to_all(iterate, "fsdp", split_axis=1, concat_axis=0, tiled=True)
    new_weights = weights_in - learn_rate * back
    return (new_weights, new_momentum)


def solution(mesh):
    placed = (P("job", "fsdp", "tp"), P("job", "fsdp", "tp"), P("job", "fsdp", "tp"))
    return jax.shard_map(
        body,
        mesh=mesh,
        in_specs=placed,
        out_specs=(P("job", "fsdp", "tp"), P("job", "fsdp", "tp")),
        check_vma=False,
    )
```

profile of v0, /device:TPU:0, one launch (start us, length us, event | category | flops | bytes accessed | tf_op | source)
XLA Modules:
  0.0 195.7 jit_solution(11048177467592807245)
XLA Ops:
  0.6 2.7 %multiply_add_fusion.5 = f32[64,32,256]{2,1,0:T(8,128)S(1)} fusion(f32[64,32,256]{2,1,0:T(8,128)} %param.3, f32[64,32,256]{2,1,0:T(8,128)} %param.4), kind=kLoop, calls=%fused_computation.8 | loop fusion | flops 1048576 | bytes 6291456 | tf_op jit(solution)/shard_map/add | solution.py:14
  3.3 54.3 %all_to_all.63 = f32[64,32,256]{2,1,0:T(8,128)S(1)} all-to-all(f32[64,32,256]{2,1,0:T(8,128)S(1)} %multiply_add_fusion.5), channel_id=1, replica_groups=mesh['fsdp'=4,'tp'=4,'job'=2] {'fsdp'}, dimensions={0} | all-to-all | bytes 4194304 | tf_op jit(solution)/shard_map/all_to_all | solution.py:15
  57.8 27.8 %all_to_all.64 = f32[16,128,256]{2,1,0:T(8,128)S(1)} all-to-all(f32[16,128,256]{2,1,0:T(8,128)S(1)} %bitcast.49), channel_id=1, replica_groups=mesh['fsdp'=4,'tp'=4,'job'=2] {'tp'}, dimensions={0} | all-to-all | bytes 4194304 | tf_op jit(solution)/shard_map/all_to_all | solution.py:16
  86.2 2.3 %fusion.2 = f32[4,128,128]{2,1,0:T(8,128)S(1)} fusion(f32[4,128,1024]{2,1,0:T(8,128)S(1)} %bitcast.45, f32[4]{0:T(128)S(1)} %add_rsqrt_fusion), kind=kOutput, calls=%fused_computation.11 | convolution fusion | flops 805830656 | bytes 2359312 | tf_op jit(solution)/shard_map/mik,mjk->mij/dot_general | solution.py:19
  88.5 0.4 fusion.10
  88.9 2.2 %multiply_add_fusion.4 = f32[4,128,1024]{2,1,0:T(8,128)S(1)} fusion(f32[4,128,1024]{2,1,0:T(8,128)S(1)} %bitcast.46, f32[4,128,128]{2,1,0:T(8,128)S(1)} %fusion.10, f32[4]{0:T(128)S(1)} %add_rsqrt_fusion), kind=kOutput, calls=%fused_computation.6 | convolution fusion | flops 807403520 | bytes 4456464 | tf_op jit(solution)/shard_map/mij,mjk->mik/dot_general | solution.py:23
  91.1 2.1 %fusion.13 = f32[4,128,128]{2,1,0:T(8,128)S(1)} fusion(f32[4,128,1024]{2,1,0:T(8,128)S(1)} %multiply_add_fusion.4), kind=kOutput, calls=%fused_computation.26 | convolution fusion | flops 805306368 | bytes 2359296 | tf_op jit(solution)/shard_map/mik,mjk->mij/dot_general | solution.py:19
  93.5 2.1 %multiply_add_fusion.3 = f32[4,128,1024]{2,1,0:T(8,128)S(1)} fusion(f32[4,128,1024]{2,1,0:T(8,128)S(1)} %multiply_add_fusion.4, f32[4,128,128]{2,1,0:T(8,128)S(1)} %fusion.9), kind=kOutput, calls=%fused_computation.5 | convolution fusion | flops 806354944 | bytes 4456448 | tf_op jit(solution)/shard_map/mij,mjk->mik/dot_general | solution.py:23
  95.6 2.1 %fusion.14 = f32[4,128,128]{2,1,0:T(8,128)S(1)} fusion(f32[4,128,1024]{2,1,0:T(8,128)S(1)} %multiply_add_fusion.3), kind=kOutput, calls=%fused_computation.27 | convolution fusion | flops 805306368 | bytes 2359296 | tf_op jit(solution)/shard_map/mik,mjk->mij/dot_general | solution.py:19
  97.6 0.4 fusion.8
  98.0 2.3 %multiply_add_fusion.2 = f32[4,128,1024]{2,1,0:T(8,128)S(1)} fusion(f32[4,128,1024]{2,1,0:T(8,128)S(1)} %multiply_add_fusion.3, f32[4,128,128]{2,1,0:T(8,128)S(1)} %fusion.8), kind=kOutput, calls=%fused_computation.4 | convolution fusion | flops 806354944 | bytes 4456448 | tf_op jit(solution)/shard_map/mij,mjk->mik/dot_general | solution.py:23
  100.3 2.0 %fusion.15 = f32[4,128,128]{2,1,0:T(8,128)S(1)} fusion(f32[4,128,1024]{2,1,0:T(8,128)S(1)} %multiply_add_fusion.2), kind=kOutput, calls=%fused_computation.28 | convolution fusion | flops 805306368 | bytes 2359296 | tf_op jit(solution)/shard_map/mik,mjk->mij/dot_general | solution.py:19
  102.4 0.4 fusion.7
  102.7 2.1 %multiply_add_fusion.1 = f32[4,128,1024]{2,1,0:T(8,128)S(1)} fusion(f32[4,128,1024]{2,1,0:T(8,128)S(1)} %multiply_add_fusion.2, f32[4,128,128]{2,1,0:T(8,128)S(1)} %fusion.7), kind=kOutput, calls=%fused_computation.3 | convolution fusion | flops 806354944 | bytes 4456448 | tf_op jit(solution)/shard_map/mij,mjk->mik/dot_general | solution.py:23
  104.8 2.0 %fusion.16 = f32[4,128,128]{2,1,0:T(8,128)S(1)} fusion(f32[4,128,1024]{2,1,0:T(8,128)S(1)} %multiply_add_fusion.1), kind=kOutput, calls=%fused_computation.29 | convolution fusion | flops 805306368 | bytes 2359296 | tf_op jit(solution)/shard_map/mik,mjk->mij/dot_general | solution.py:19
  107.3 2.1 %multiply_add_fusion = f32[4,128,1024]{2,1,0:T(8,128)S(1)} fusion(f32[4,128,1024]{2,1,0:T(8,128)S(1)} %multiply_add_fusion.1, f32[4,128,128]{2,1,0:T(8,128)S(1)} %fusion.6), kind=kOutput, calls=%fused_computation.2 | convolution fusion | flops 806354944 | bytes 4456448 | tf_op jit(solution)/shard_map/mij,mjk->mik/dot_general | solution.py:23
  109.3 1.8 copy.19
  111.2 26.5 %all_to_all.65 = f32[4,128,1024]{1,0,2:T(4,128)S(1)} all-to-all(f32[4,128,1024]{1,0,2:T(4,128)} %copy.19), channel_id=1, replica_groups=mesh['fsdp'=4,'tp'=4,'job'=2] {'tp'}, dimensions={2} | all-to-all | bytes 4194304 | tf_op jit(solution)/shard_map/all_to_all | solution.py:26
  137.8 1.8 copy.21
  139.6 2.8 %copy.22 = f32[16,128,256]{2,0,1:T(8,128)S(1)} copy(f32[16,128,256]{2,1,0:T(8,128)} %bitcast.51) | data formatting | bytes 4194304 | tf_op jit(solution)/shard_map/all_to_all | solution.py:26
  142.4 48.6 %all_to_all.66 = f32[16,128,256]{2,0,1:T(8,128)S(1)} all-to-all(f32[16,128,256]{2,0,1:T(8,128)S(1)} %copy.22), channel_id=1, replica_groups=mesh['fsdp'=4,'tp'=4,'job'=2] {'fsdp'}, dimensions={1} | all-to-all | bytes 4194304 | tf_op jit(solution)/shard_map/all_to_all | solution.py:27
  191.0 1.4 copy_multiply_fusion
  192.5 1.4 copy-done.1
  194.0 1.7 bitcast_subtract_fusion
  (11 shorter events, 1.8 us)
Async XLA Ops:
  3.3 54.4 %copy-start = (f32[64,32,256]{2,1,0:T(8,128)}, f32[64,32,256]{2,1,0:T(8,128)S(1)}, u32[]{:S(2)}) copy-start(f32[64,32,256]{2,1,0:T(8,128)S(1)} %multiply_add_fusion.5) | copy-start | bytes 6291460
  192.4 1.6 copy-start.1
where the time goes:
time: 196 us
  blocking collectives  157 us (80%)
  matrix products  23 us (12%)
  local copies, waits for them, and re-layouts  8.59 us (4%)
  other arithmetic  6.08 us (3%)
    all_to_all x1, blocking collectives, body(): lax.all_to_all(new_momentum, 'fsdp', split_axis=0, concat_axis=1, tiled=T...  54.3 us
    all_to_all x1, blocking collectives, body(): lax.all_to_all(iterate, 'fsdp', split_axis=1, concat_axis=0, tiled=True)  48.6 us
    all_to_all x1, blocking collectives, body(): whole = lax.all_to_all(moved, 'tp', split_axis=0, concat_axis=2, tiled=True)  27.8 us
    all_to_all x1, blocking collectives, body(): lax.all_to_all(iterate, 'tp', split_axis=2, concat_axis=0, tiled=True)  26.5 us
    dot_general x5, matrix products, body(): jnp.einsum('mij,mjk->mik', mixed, iterate, precision=lax.Precision.HIGHEST)  10.7 us
    dot_general x5, matrix products, body(): jnp.einsum('mik,mjk->mij', iterate, iterate, precision=lax.Precision.HIGH...  10.5 us
    all_to_all x3, local copies, waits for them, and re-layouts, body(): lax.all_to_all(iterate, 'tp', split_axis=2, concat_axis=0, tiled=True)  4.76 us

commit v1 on v0

v1 whole, which is shorter than its diff:
```python
import functools

import jax
import jax.numpy as jnp
from jax import lax
from jax.experimental import pallas as pl
from jax.experimental.pallas import tpu as pltpu
from jax.sharding import PartitionSpec as P

ITERS = 5


hold_rate = 0.9
learn_rate = 0.8

COEF_A, COEF_B, COEF_C = 3.4445, -4.775, 2.0315
MESH = pl.DeviceIdType.MESH
HIGHEST = lax.Precision.HIGHEST


def dot(a, b, contract=((1,), (0,))):
    return lax.dot_general(
        a, b, (contract, ((), ())), precision=HIGHEST, preferred_element_type=jnp.float32
    )


def factor_of(gram):
    side = gram.shape[0]
    rows = lax.broadcasted_iota(jnp.int32, (side, side), 0)
    eye = rows == lax.broadcasted_iota(jnp.int32, (side, side), 1)
    total = jnp.sum(jnp.where(eye, gram, 0.0), axis=(0, 1), keepdims=True)
    scale = lax.rsqrt(total + 1e-06)

    def mixed_of(a):
        return COEF_B * a + COEF_C * dot(a, a)

    def step(_, carry):
        a, q = carry
        mixed = mixed_of(a)
        half = COEF_A * a + dot(mixed, a)
        return COEF_A * half + dot(half, mixed), COEF_A * q + dot(mixed, q)

    a = gram * scale * scale
    q = jnp.where(eye, jnp.broadcast_to(scale, gram.shape), 0.0)
    a, q = lax.fori_loop(0, ITERS - 1, step, (a, q))
    return COEF_A * q + dot(mixed_of(a), q)


def kernel(nf, nt, chunks, mom, out, xbuf, gsend, grecv, qrecv, ybuf, fsend, frecv, gs, gr, qs, qr, bsend, brecv, own):
    me_f, me_t = lax.axis_index("fsdp"), lax.axis_index("tp")
    mats, rows, _ = mom.shape
    share = mats // nf
    per = share // chunks
    each = per // nt

    barrier = pltpu.get_barrier_semaphore()
    for d in range(1, nf):
        pl.semaphore_signal(barrier, inc=1, device_id={"fsdp": lax.rem(me_f + d, nf)}, device_id_type=MESH)
    for d in range(1, nt):
        pl.semaphore_signal(barrier, inc=1, device_id={"tp": lax.rem(me_t + d, nt)}, device_id_type=MESH)
    pl.semaphore_wait(barrier, nf + nt - 2)

    my_rows = pl.ds(pl.multiple_of(me_f * rows, rows), rows)

    def there(c, d):
        peer = lax.rem(me_f + d, nf)
        return pltpu.make_async_remote_copy(
            src_ref=mom.at[pl.ds(peer * share + c * per, per)],
            dst_ref=xbuf.at[pl.ds(c * per, per), my_rows, :],
            send_sem=fsend.at[c, d - 1], recv_sem=frecv.at[c, d - 1],
            device_id={"fsdp": peer}, device_id_type=MESH,
        )

    def stay(c):
        return pltpu.make_async_copy(
            mom.at[pl.ds(me_f * share + c * per, per)],
            xbuf.at[pl.ds(c * per, per), my_rows, :], own.at[0, c],
        )

    def back(c, d):
        peer = lax.rem(me_f + d, nf)
        theirs = pl.ds(pl.multiple_of(peer * rows, rows), rows)
        return pltpu.make_async_remote_copy(
            src_ref=ybuf.at[pl.ds(c * per, per), theirs, :],
            dst_ref=out.at[pl.ds(me_f * share + c * per, per)],
            send_sem=bsend.at[c, d - 1], recv_sem=brecv.at[c, d - 1],
            device_id={"fsdp": peer}, device_id_type=MESH,
        )

    def keep(c):
        return pltpu.make_async_copy(
            ybuf.at[pl.ds(c * per, per), my_rows, :],
            out.at[pl.ds(me_f * share + c * per, per)], own.at[1, c],
        )

    def gram_copy(c, d):
        return pltpu.make_async_remote_copy(
            src_ref=gsend.at[c, d - 1], dst_ref=grecv.at[c, d],
            send_sem=gs.at[c, d - 1], recv_sem=gr.at[c, d - 1],
            device_id={"tp": lax.rem(me_t + d, nt)}, device_id_type=MESH,
        )

    def factor_copy(c, d):
        return pltpu.make_async_remote_copy(
            src_ref=qrecv.at[c, 0], dst_ref=qrecv.at[c, d],
            send_sem=qs.at[c, d - 1], recv_sem=qr.at[c, d - 1],
            device_id={"tp": lax.rem(me_t + d, nt)}, device_id_type=MESH,
        )

    def grams(c):
        stay(c).wait()
        for d in range(1, nf):
            there(c, d).wait_recv()
        for d in list(range(1, nt)) + [0]:
            first = c * per + lax.rem(me_t + d, nt) * each
            for e in range(each):
                x = xbuf[first + e]
                g = dot(x, x, ((1,), (1,)))
                if d == 0:
                    grecv[c, 0, e] = g
                else:
                    gsend[c, d - 1, e] = g
            if d > 0:
                gram_copy(c, d).start()

    def factors(c):
        for d in range(1, nt):
            gram_copy(c, d).wait_recv()
        for e in range(each):
            g = grecv[c, 0, e]
            for d in range(1, nt):
                g = g + grecv[c, d, e]
            qrecv[c, 0, e] = factor_of(g)
        for d in range(1, nt):
            factor_copy(c, d).start()

    def apply(c):
        for d in range(nt):
            if d > 0:
                factor_copy(c, d).wait_recv()
            first = c * per + lax.rem(me_t - d + nt, nt) * each
            for e in range(each):
                ybuf[first + e] = dot(qrecv[c, d, e], xbuf[first + e])
        for d in range(1, nf):
            back(c, d).start()
        keep(c).start()

    for c in range(chunks):
        for d in range(1, nf):
            there(c, d).start()
        stay(c).start()

    for c in range(chunks + 1):
        if c < chunks:
            grams(c)
        if c > 0:
            apply(c - 1)
        if c < chunks:
            factors(c)

    for c in range(chunks):
        keep(c).wait()
        for d in range(1, nf):
            there(c, d).wait_send()
            back(c, d).wait_send()
            back(c, d).wait_recv()
        for d in range(1, nt):
            gram_copy(c, d).wait_send()
            factor_copy(c, d).wait_send()


def orthogonal(nf, nt, new_momentum):
    mats, rows, wide = new_momentum.shape
    side, share = rows * nf, mats // nf
    most = share // nt
    chunks = max(k for k in range(1, 5) if most % k == 0)
    per = share // chunks
    each = per // nt
    vmem, dma = pltpu.VMEM, pltpu.SemaphoreType.DMA
    return pl.pallas_call(
        functools.partial(kernel, nf, nt, chunks),
        out_shape=jax.ShapeDtypeStruct(new_momentum.shape, jnp.float32),
        in_specs=[pl.BlockSpec(memory_space=pltpu.VMEM)],
        out_specs=pl.BlockSpec(memory_space=pltpu.VMEM),
        scratch_shapes=[
            vmem((share, side, wide), jnp.float32),
            vmem((chunks, nt - 1, each, side, side), jnp.float32),
            vmem((chunks, nt, each, side, side), jnp.float32),
            vmem((chunks, nt, each, side, side), jnp.float32),
            vmem((share, side, wide), jnp.float32),
            dma((chunks, nf - 1)), dma((chunks, nf - 1)),
            dma((chunks, nt - 1)), dma((chunks, nt - 1)),
            dma((chunks, nt - 1)), dma((chunks, nt - 1)),
            dma((chunks, nf - 1)), dma((chunks, nf - 1)),
            dma((2, chunks)),
        ],
        compiler_params=pltpu.CompilerParams(
            collective_id=0, has_side_effects=True, vmem_limit_bytes=32 * 2**20
        ),
    )(new_momentum)


def orthogonal_plain(new_momentum):
    moved = lax.all_to_all(new_momentum, "fsdp", split_axis=0, concat_axis=1, tiled=True)
    gram = lax.dot_general(moved, moved, (((2,), (2,)), ((0,), (0,))), precision=HIGHEST)
    gram = lax.psum_scatter(gram, "tp", scatter_dimension=0, tiled=True)
    factors = lax.all_gather(jax.vmap(factor_of)(gram), "tp", axis=0, tiled=True)
    whole = lax.dot_general(factors, moved, (((2,), (1,)), ((0,), (0,))), precision=HIGHEST)
    return lax.all_to_all(whole, "fsdp", split_axis=1, concat_axis=0, tiled=True)


def body(nf, nt, slopes_in, moments_in, weights_in):
    new_momentum = hold_rate * moments_in + slopes_in
    rows, wide = new_momentum.shape[1:]
    if rows % 8 == 0 and wide % 128 == 0:
        iterate = orthogonal(nf, nt, new_momentum)
    else:
        iterate = orthogonal_plain(new_momentum)
    new_weights = weights_in - learn_rate * iterate
    return (new_weights, new_momentum)


def solution(mesh):
    placed = (P("job", "fsdp", "tp"), P("job", "fsdp", "tp"), P("job", "fsdp", "tp"))
    return jax.shard_map(
        functools.partial(body, mesh.shape["fsdp"], mesh.shape["tp"]),
        mesh=mesh,
        in_specs=placed,
        out_specs=(P("job", "fsdp", "tp"), P("job", "fsdp", "tp")),
        check_vma=False,
    )
```

time: 196 us -> 102 us (0.52)
  blocking collectives: 157 us -> 0 us
  Pallas kernels: 0 us -> 96.1 us
  matrix products: 23 us -> 0 us
  local copies, waits for them, and re-layouts: 8.59 us -> 0.01 us
    all_to_all x4 -> x0, blocking collectives: 157 us -> none  [the longest x1 54.3 us: body(): lax.all_to_all(new_momentum, 'fsdp', split_axis=0, concat_axis=1, tiled=T...]
    pallas_call x0 -> x1, Pallas kernels: none -> 96.1 us  [orthogonal(): pl.pallas_call(functools.partial(kernel, nf, nt, chunks), out_shape=jax.S...]
    dot_general x15 -> x0, matrix products: 23 us -> none  [the longest x5 10.7 us: body(): jnp.einsum('mij,mjk->mik', mixed, iterate, precision=lax.Precision.HIGHEST)]
    all_to_all x5 -> x0, local copies, waits for them, and re-layouts: 5.2 us -> none  [the longest x3 4.76 us: body(): lax.all_to_all(iterate, 'tp', split_axis=2, concat_axis=0, tiled=True)]
where the time goes in v1:
time: 102 us
  Pallas kernels  96.1 us (94%)
  other arithmetic  4.77 us (5%)
    pallas_call x1, Pallas kernels, orthogonal(): pl.pallas_call(functools.partial(kernel, nf, nt, chunks), out_shape=jax.S...  96.1 us
    add x1, other arithmetic, body(): new_momentum = hold_rate * moments_in + slopes_in  2.83 us

profile of v1, /device:TPU:0, one launch (start us, length us, event | category | flops | bytes accessed | tf_op | source)
XLA Modules:
  0.0 101.5 jit_solution(2302477486121986462)
XLA Ops:
  0.6 2.8 %multiply_add_fusion.mom = f32[64,32,256]{2,1,0:T(8,128)S(1)} fusion(f32[64,32,256]{2,1,0:T(8,128)} %param.3, f32[64,32,256]{2,1,0:T(8,128)} %param.4), kind=kLoop, calls=%fused_computation.1 | loop fusion | flops 1048576 | bytes 6291456 | tf_op jit(solution)/shard_map/add | solution.py:213
  3.5 0.0 copy-start
  3.5 0.0 copy-start.1
  3.5 96.1 %shard_map.50 = f32[64,32,256]{2,1,0:T(8,128)S(1)} custom-call(f32[64,32,256]{2,1,0:T(8,128)S(1)} %multiply_add_fusion.mom), custom_call_target="tpu_custom_call" | custom-call | tf_op jit(solution)/shard_map/pallas_call | solution.py:180
  99.6 0.0 copy-done.1
  99.6 1.9 %multiply_subtract_fusion = f32[64,32,256]{2,1,0:T(8,128)} fusion(f32[64,32,256]{2,1,0:T(8,128)S(1)} %copy-done.1, f32[64,32,256]{2,1,0:T(8,128)S(1)} %shard_map.50), kind=kLoop, calls=%fused_computation | loop fusion | flops 1048576 | bytes 6291456 | tf_op jit(solution)/shard_map/sub | solution.py:219
  101.5 0.0 copy-done
Async XLA Ops:
  3.5 98.1 %copy-start = (f32[64,32,256]{2,1,0:T(8,128)}, f32[64,32,256]{2,1,0:T(8,128)S(1)}, u32[]{:S(2)}) copy-start(f32[64,32,256]{2,1,0:T(8,128)S(1)} %multiply_add_fusion.mom) | copy-start | bytes 6291460
  3.5 96.1 %copy-start.1 = (f32[64,32,256]{2,1,0:T(8,128)S(1)}, f32[64,32,256]{2,1,0:T(8,128)}, u32[]{:S(2)}) copy-start(f32[64,32,256]{2,1,0:T(8,128)} %param.5) | copy-start | bytes 6291460

commit v2 on v1

--- a/solution.py
+++ b/solution.py
@@ -46,7 +46,7 @@
     return COEF_A * q + dot(mixed_of(a), q)
 
 
-def kernel(nf, nt, chunks, mom, out, xbuf, gsend, grecv, qrecv, ybuf, fsend, frecv, gs, gr, qs, qr, bsend, brecv, own):
+def kernel(nf, nt, chunks, slopes, moments, weights, new, mom, out, wbuf, sbuf, mbuf, xbuf, gsend, grecv, qrecv, ybuf, fsend, frecv, gs, gr, qs, qr, bsend, brecv, own, loads):
     me_f, me_t = lax.axis_index("fsdp"), lax.axis_index("tp")
     mats, rows, _ = mom.shape
     share = mats // nf
@@ -58,7 +58,24 @@
         pl.semaphore_signal(barrier, inc=1, device_id={"fsdp": lax.rem(me_f + d, nf)}, device_id_type=MESH)
     for d in range(1, nt):
         pl.semaphore_signal(barrier, inc=1, device_id={"tp": lax.rem(me_t + d, nt)}, device_id_type=MESH)
-    pl.semaphore_wait(barrier, nf + nt - 2)
+
+    order = [(c, d) for c in range(chunks) for d in list(range(1, nf)) + [0]]
+
+    def block(c, d):
+        return pl.ds(lax.rem(me_f + d, nf) * share + c * per, per)
+
+    def load(c, d):
+        here = block(c, d)
+        return (
+            pltpu.make_async_copy(slopes.at[here], sbuf.at[here], loads.at[0, c, d]),
+            pltpu.make_async_copy(moments.at[here], mbuf.at[here], loads.at[1, c, d]),
+        )
+
+    for c, d in order:
+        for copy in load(c, d):
+            copy.start()
+    fetch = pltpu.make_async_copy(weights, wbuf, own.at[2, 0])
+    fetch.start()
 
     my_rows = pl.ds(pl.multiple_of(me_f * rows, rows), rows)
 
@@ -145,10 +162,25 @@
             back(c, d).start()
         keep(c).start()
 
-    for c in range(chunks):
-        for d in range(1, nf):
+    def send(c, d):
+        if d > 0:
             there(c, d).start()
-        stay(c).start()
+        else:
+            stay(c).start()
+
+    def momentum(c, d):
+        for copy in load(c, d):
+            copy.wait()
+        here = block(c, d)
+        mom[here] = hold_rate * mbuf[here] + sbuf[here]
+
+    for k, (c, d) in enumerate(order):
+        momentum(c, d)
+        if k == 0:
+            pl.semaphore_wait(barrier, nf + nt - 2)
+        else:
+            send(*order[k - 1])
+    send(*order[-1])
 
     for c in range(chunks + 1):
         if c < chunks:
@@ -158,31 +190,56 @@
         if c < chunks:
             factors(c)
 
+    fetch.wait()
     for c in range(chunks):
-        keep(c).wait()
+        for d in range(nf):
+            if d > 0:
+                back(c, d).wait_recv()
+            else:
+                keep(c).wait()
+            here = pl.ds(lax.rem(me_f - d + nf, nf) * share + c * per, per)
+            new[here] = wbuf[here] - learn_rate * out[here]
+
+    for c in range(chunks):
         for d in range(1, nf):
             there(c, d).wait_send()
             back(c, d).wait_send()
-            back(c, d).wait_recv()
         for d in range(1, nt):
             gram_copy(c, d).wait_send()
             factor_copy(c, d).wait_send()
 
 
-def orthogonal(nf, nt, new_momentum):
-    mats, rows, wide = new_momentum.shape
+def finish(new, mom, new_out, mom_out, sems):
+    copies = []
+    for k, (src, dst) in enumerate(((mom, mom_out), (new, new_out))):
+        copies.append(pltpu.make_async_copy(src, dst, sems.at[k]))
+    for copy in copies:
+        copy.start()
+    for copy in copies:
+        copy.wait()
+
+
+def stepped(nf, nt, slopes_in, moments_in, weights_in):
+    mats, rows, wide = slopes_in.shape
     side, share = rows * nf, mats // nf
     most = share // nt
     chunks = max(k for k in range(1, 5) if most % k == 0)
     per = share // chunks
     each = per // nt
     vmem, dma = pltpu.VMEM, pltpu.SemaphoreType.DMA
-    return pl.pallas_call(
+    shape = jax.ShapeDtypeStruct(slopes_in.shape, jnp.float32)
+    held = [pl.BlockSpec(memory_space=pltpu.VMEM)] * 2
+    far = [pl.BlockSpec(memory_space=pltpu.HBM)]
+    results = pl.pallas_call(
         functools.partial(kernel, nf, nt, chunks),
-        out_shape=jax.ShapeDtypeStruct(new_momentum.shape, jnp.float32),
-        in_specs=[pl.BlockSpec(memory_space=pltpu.VMEM)],
-        out_specs=pl.BlockSpec(memory_space=pltpu.VMEM),
+        out_shape=[shape] * 2,
+        in_specs=far * 3,
+        out_specs=held,
         scratch_shapes=[
+            vmem(slopes_in.shape, jnp.float32),
+            vmem(slopes_in.shape, jnp.float32),
+            vmem(slopes_in.shape, jnp.float32),
+            vmem(slopes_in.shape, jnp.float32),
             vmem((share, side, wide), jnp.float32),
             vmem((chunks, nt - 1, each, side, side), jnp.float32),
             vmem((chunks, nt, each, side, side), jnp.float32),
@@ -192,12 +249,20 @@
             dma((chunks, nt - 1)), dma((chunks, nt - 1)),
             dma((chunks, nt - 1)), dma((chunks, nt - 1)),
             dma((chunks, nf - 1)), dma((chunks, nf - 1)),
-            dma((2, chunks)),
+            dma((3, chunks)), dma((2, chunks, nf)),
         ],
         compiler_params=pltpu.CompilerParams(
             collective_id=0, has_side_effects=True, vmem_limit_bytes=32 * 2**20
         ),
-    )(new_momentum)
+    )(*(pltpu.with_memory_space_constraint(x, pltpu.HBM) for x in (slopes_in, moments_in, weights_in)))
+    return pl.pallas_call(
+        finish,
+        out_shape=[shape] * 2,
+        in_specs=held,
+        out_specs=far * 2,
+        scratch_shapes=[dma((2,))],
+        compiler_params=pltpu.CompilerParams(vmem_limit_bytes=2**20),
+    )(*results)
 
 
 def orthogonal_plain(new_momentum):
@@ -210,13 +275,11 @@
 
 
 def body(nf, nt, slopes_in, moments_in, weights_in):
+    rows, wide = slopes_in.shape[1:]
+    if rows % 8 == 0 and wide % 128 == 0:
+        return stepped(nf, nt, slopes_in, moments_in, weights_in)
     new_momentum = hold_rate * moments_in + slopes_in
-    rows, wide = new_momentum.shape[1:]
-    if rows % 8 == 0 and wide % 128 == 0:
-        iterate = orthogonal(nf, nt, new_momentum)
-    else:
-        iterate = orthogonal_plain(new_momentum)
-    new_weights = weights_in - learn_rate * iterate
+    new_weights = weights_in - learn_rate * orthogonal_plain(new_momentum)
     return (new_weights, new_momentum)
 
 

time: 102 us -> 99.4 us (0.975)
  other arithmetic: 4.77 us -> 0 us
  Pallas kernels: 96.1 us -> 98.6 us
    add x1 -> x0, other arithmetic: 2.83 us -> none  [body(): new_momentum = hold_rate * moments_in + slopes_in]
    pallas_call x1 -> x2, Pallas kernels: 96.1 us -> 98.6 us  [the longest x1 96.5 us: stepped(): pl.pallas_call(functools.partial(kernel, nf, nt, chunks), out_shape=[shap...]
    sub x1 -> x0, other arithmetic: 1.94 us -> none  [body(): new_weights = weights_in - learn_rate * iterate]
where the time goes in v2:
time: 99.4 us; the launch traced here: 99.2 us
  Pallas kernels  98.6 us (99%)
    pallas_call x1, Pallas kernels, stepped(): pl.pallas_call(functools.partial(kernel, nf, nt, chunks), out_shape=[shap...  96.5 us
    pallas_call x1, Pallas kernels, stepped(): pl.pallas_call(finish, out_shape=[shape] * 2, in_specs=held, out_specs=fa...  2.03 us

profile of v2, /device:TPU:0, one launch (start us, length us, event | category | flops | bytes accessed | tf_op | source)
XLA Modules:
  0.0 99.2 jit_solution(1462658984015305055)
XLA Ops:
  0.6 96.5 %shard_map.50 = (f32[64,32,256]{2,1,0:T(8,128)S(1)}, f32[64,32,256]{2,1,0:T(8,128)S(1)}) custom-call(f32[64,32,256]{2,1,0:T(8,128)} %slopes.1, f32[64,32,256]{2,1,0:T(8,128)} %moments.1, f32[64,32,256]{2,1,0:T(8,128)} %weights.1), custom_call_target="tpu_custom_call" | custom-call | tf_op jit(solution)/shard_map/pallas_call | solution.py:233
  97.2 2.0 %shard_map.51 = (f32[64,32,256]{2,1,0:T(8,128)}, f32[64,32,256]{2,1,0:T(8,128)}) custom-call(f32[64,32,256]{2,1,0:T(8,128)S(1)} %get-tuple-element.4.new, f32[64,32,256]{2,1,0:T(8,128)S(1)} %get-tuple-element.5.mom), custom_call_target="tpu_custom_call" | custom-call | tf_op jit(solution)/shard_map/pallas_call | solution.py:258

commit v3 on v2

--- a/solution.py
+++ b/solution.py
@@ -46,6 +46,17 @@
     return COEF_A * q + dot(mixed_of(a), q)
 
 
+def partner(me, d, n):
+    if n & (n - 1):
+        return lax.rem(me + d, n), lax.rem(me - d + n, n)
+    other, bit = 0, 1
+    while bit < n:
+        mine = lax.rem(lax.div(me, bit), 2)
+        other = other + bit * (1 - mine if d & bit else mine)
+        bit *= 2
+    return other, other
+
+
 def kernel(nf, nt, chunks, slopes, moments, weights, new, mom, out, wbuf, sbuf, mbuf, xbuf, gsend, grecv, qrecv, ybuf, fsend, frecv, gs, gr, qs, qr, bsend, brecv, own, loads):
     me_f, me_t = lax.axis_index("fsdp"), lax.axis_index("tp")
     mats, rows, _ = mom.shape
@@ -54,15 +65,17 @@
     each = per // nt
 
     barrier = pltpu.get_barrier_semaphore()
+    pairs = [partner(me_f, d, nf) for d in range(nf)]
+    goal, source = [a for a, _ in pairs], [b for _, b in pairs]
     for d in range(1, nf):
-        pl.semaphore_signal(barrier, inc=1, device_id={"fsdp": lax.rem(me_f + d, nf)}, device_id_type=MESH)
+        pl.semaphore_signal(barrier, inc=1, device_id={"fsdp": goal[d]}, device_id_type=MESH)
     for d in range(1, nt):
         pl.semaphore_signal(barrier, inc=1, device_id={"tp": lax.rem(me_t + d, nt)}, device_id_type=MESH)
 
-    order = [(c, d) for c in range(chunks) for d in list(range(1, nf)) + [0]]
+    order = [(c, d) for c in range(chunks) for d in (range(nf - 1, -1, -1) if c == 0 else range(nf))]
 
     def block(c, d):
-        return pl.ds(lax.rem(me_f + d, nf) * share + c * per, per)
+        return pl.ds(goal[d] * share + c * per, per)
 
     def load(c, d):
         here = block(c, d)
@@ -71,16 +84,19 @@
             pltpu.make_async_copy(moments.at[here], mbuf.at[here], loads.at[1, c, d]),
         )
 
-    for c, d in order:
-        for copy in load(c, d):
-            copy.start()
+    def begin(chunk):
+        for c, d in order:
+            if c == chunk:
+                for copy in load(c, d):
+                    copy.start()
+
+    begin(0)
     fetch = pltpu.make_async_copy(weights, wbuf, own.at[2, 0])
-    fetch.start()
 
     my_rows = pl.ds(pl.multiple_of(me_f * rows, rows), rows)
 
     def there(c, d):
-        peer = lax.rem(me_f + d, nf)
+        peer = goal[d]
         return pltpu.make_async_remote_copy(
             src_ref=mom.at[pl.ds(peer * share + c * per, per)],
             dst_ref=xbuf.at[pl.ds(c * per, per), my_rows, :],
@@ -95,7 +111,7 @@
         )
 
     def back(c, d):
-        peer = lax.rem(me_f + d, nf)
+        peer = goal[d]
         theirs = pl.ds(pl.multiple_of(peer * rows, rows), rows)
         return pltpu.make_async_remote_copy(
             src_ref=ybuf.at[pl.ds(c * per, per), theirs, :],
@@ -180,7 +196,10 @@
             pl.semaphore_wait(barrier, nf + nt - 2)
         else:
             send(*order[k - 1])
+        if k % nf == nf - 1 and c + 1 < chunks:
+            begin(c + 1)
     send(*order[-1])
+    fetch.start()
 
     for c in range(chunks + 1):
         if c < chunks:
@@ -197,7 +216,7 @@
                 back(c, d).wait_recv()
             else:
                 keep(c).wait()
-            here = pl.ds(lax.rem(me_f - d + nf, nf) * share + c * per, per)
+            here = pl.ds(source[d] * share + c * per, per)
             new[here] = wbuf[here] - learn_rate * out[here]
 
     for c in range(chunks):

time: 99.4 us -> 99.5 us (level)
  no operation moved by 1% of the time
where the time goes in v3:
time: 99.5 us; the launch traced here: 99.3 us
  Pallas kernels  98.6 us (99%)
    pallas_call x1, Pallas kernels, stepped(): pl.pallas_call(functools.partial(kernel, nf, nt, chunks), out_shape=[shap...  96.6 us
    pallas_call x1, Pallas kernels, stepped(): pl.pallas_call(finish, out_shape=[shape] * 2, in_specs=held, out_specs=fa...  2.03 us

profile of v3, /device:TPU:0, one launch (start us, length us, event | category | flops | bytes accessed | tf_op | source)
XLA Modules:
  0.0 99.3 jit_solution(12512063426954769322)
XLA Ops:
  0.6 96.6 %shard_map.50 = (f32[64,32,256]{2,1,0:T(8,128)S(1)}, f32[64,32,256]{2,1,0:T(8,128)S(1)}) custom-call(f32[64,32,256]{2,1,0:T(8,128)} %slopes.1, f32[64,32,256]{2,1,0:T(8,128)} %moments.1, f32[64,32,256]{2,1,0:T(8,128)} %weights.1), custom_call_target="tpu_custom_call" | custom-call | tf_op jit(solution)/shard_map/pallas_call | solution.py:252
  97.2 2.0 %shard_map.51 = (f32[64,32,256]{2,1,0:T(8,128)}, f32[64,32,256]{2,1,0:T(8,128)}) custom-call(f32[64,32,256]{2,1,0:T(8,128)S(1)} %get-tuple-element.4.new, f32[64,32,256]{2,1,0:T(8,128)S(1)} %get-tuple-element.5.mom), custom_call_target="tpu_custom_call" | custom-call | tf_op jit(solution)/shard_map/pallas_call | solution.py:277
